TPU v7x, 32 devices: a whole 2x2x4 slice. The times are simulated.
32 devices in a mesh: section: 4 (over y, x), seq: 8 (over z, core).
Axes of the slice: x: 2, y: 2, z: 4, core: 2. Of those that a mesh axis runs over, the one named last changes fastest.
Arguments:
- stream: bfloat16 [4, 1024, 4096], P('section', 'seq'), may hold values from -4 to 4
- queries: bfloat16 [4, 1024, 4096], P('section', 'seq')
- span_kv: bfloat16 [4, 2, 1024, 512], P('section', None, 'seq')
- cache_kv: bfloat16 [4, 2, 1024, 512], P('section', None, 'seq'), may hold values from -6 to 6
- cache_len: int32 [8], replicated, may hold values from 48 to 80, as said below
- context_start: int32 [1], replicated, may hold values from 1 to 1024
- block_table: int32 [8, 8], replicated, may hold values from 0 to 1, as said below
Outputs:
- handed: bfloat16 [4, 1024, 4096], P('section', 'seq')
Inputs may be any that keep to these rules, and one draw needn't show every extreme that they name: `cache_len`: some index holds exactly 80 live slots. `block_table`: the diagonal is 1 and every entry above it is 0.
All inputs are finite; a program needn't handle non-finite values.
Results may differ from a plain program's by a relative error of at most 0.006.
Values may be sent and summed in bfloat16 or wider, within the bound.
A program may use at most 64 MiB of HBM per device.

v0:
```python
import math

import jax
import jax.numpy as jnp
from jax import lax
from jax.sharding import PartitionSpec as P

HEAD_DIM = 128
LIVE_MAX = 80


def passed_along(value, axis, steps):
    count = lax.axis_size(axis)
    pairs = [(source, (source + steps) % count) for source in range(count)]
    return lax.ppermute(value, axis, pairs)


def shards(stream, queries, span_kv, cache_kv, cache_len, context_start, block_table):
    seq_count = lax.axis_size("seq")
    seq_index = lax.axis_index("seq")
    query_rows = queries[0]
    tok_rows = query_rows.shape[0]
    query_width = query_rows.shape[1]
    key_width = span_kv.shape[3]
    kv_count = key_width // HEAD_DIM
    group_size = query_width // key_width
    grouped = query_rows.reshape(tok_rows, kv_count, group_size, HEAD_DIM).transpose(1, 0, 2, 3)
    grouped = grouped.reshape(kv_count, tok_rows * group_size, HEAD_DIM)
    score_scale = 1.0 / math.sqrt(HEAD_DIM)
    slot_rows = cache_kv.shape[2]
    first_visible = slot_rows * seq_count - context_start[0]
    table_row = lax.dynamic_index_in_dim(block_table, seq_index, 0, keepdims=False)
    query_pos = seq_index * tok_rows + jnp.arange(tok_rows, dtype=jnp.int32)
    shard_ids = jnp.arange(seq_count, dtype=jnp.int32)

    def update(state_carry, key_values, allowed):
        row_top, row_total, accumulated = state_carry
        block_rows = key_values.shape[1]
        key_heads = key_values[0].reshape(block_rows, kv_count, HEAD_DIM)
        value_heads = key_values[1].reshape(block_rows, kv_count, HEAD_DIM)
        scores = (
            jnp.einsum("kqd,rkd->kqr", grouped, key_heads, preferred_element_type=jnp.float32)
            * score_scale
        )
        masked = jnp.where(allowed[None], scores, -1e30)
        new_top = jnp.maximum(row_top, jnp.max(masked, -1))
        weights = jnp.where(allowed[None], jnp.exp(scores - new_top[..., None]), 0.0)
        factor = jnp.exp(row_top - new_top)
        new_total = row_total * factor + jnp.sum(weights, -1)
        product = jnp.einsum(
            "kqr,rkd->kqd",
            weights.astype(jnp.bfloat16),
            value_heads,
            preferred_element_type=jnp.float32,
        )
        return (new_top, new_total, accumulated * factor[..., None] + product)

    def run_blocks(state_carry, shard_piece, shard_len, mask_rule):
        pairs = shard_piece[0]
        piece_rows = pairs.shape[1]
        shard_total = piece_rows // shard_len
        wanted = max(1, 512 // shard_len)
        shards_per = math.gcd(shard_total, wanted)
        block_rows = shards_per * shard_len
        block_count = piece_rows // block_rows

        def one_block(block, inner_carry):
            key_values = lax.dynamic_slice_in_dim(pairs, block * block_rows, block_rows, 1)
            allowed = mask_rule(block * block_rows, block_rows)
            return update(inner_carry, key_values, allowed)

        return lax.fori_loop(0, block_count, one_block, state_carry)

    def cache_rule_for(shard_len):
        row_ids = jnp.arange(shard_len * seq_count, dtype=jnp.int32)
        owner = row_ids // shard_len
        slot_index = row_ids % shard_len
        live_counts = jnp.sum(
            jnp.where(owner[:, None] == shard_ids[None, :], cache_len[None, :], 0), 1
        )
        position = owner * slot_rows + slot_index
        cache_open = (slot_index < live_counts) & (position >= first_visible)

        def cache_rule(block_first, block_rows):
            return lax.dynamic_slice_in_dim(cache_open, block_first, block_rows, 0)[None, :]

        return cache_rule

    key_all = jnp.arange(tok_rows * seq_count, dtype=jnp.int32)
    key_owner = key_all // tok_rows
    table_open = (
        jnp.sum(jnp.where(key_owner[:, None] == shard_ids[None, :], table_row[None, :], 0), 1) == 1
    )

    def span_rule(block_first, block_rows):
        key_ids = block_first + jnp.arange(block_rows, dtype=jnp.int32)
        table_hits = lax.dynamic_slice_in_dim(table_open, block_first, block_rows, 0)
        allowed = (key_ids[None, :] <= query_pos[:, None]) & table_hits[None, :]
        allowed = jnp.broadcast_to(allowed[:, None, :], (tok_rows, group_size, block_rows))
        return allowed.reshape(tok_rows * group_size, block_rows)

    start_carry = (
        jnp.full((kv_count, tok_rows * group_size), -1e30, jnp.float32),
        jnp.zeros((kv_count, tok_rows * group_size), jnp.float32),
        jnp.zeros((kv_count, tok_rows * group_size, HEAD_DIM), jnp.float32),
    )
    live_slots = cache_kv[:, :, :LIVE_MAX]
    live_rule = cache_rule_for(LIVE_MAX)
    after_cache = run_blocks(
        start_carry, lax.all_gather(live_slots, "seq", axis=2, tiled=True), LIVE_MAX, live_rule
    )
    row_top, row_total, accumulated = run_blocks(
        after_cache, lax.all_gather(span_kv, "seq", axis=2, tiled=True), tok_rows, span_rule
    )
    mixed = accumulated / row_total[..., None]
    mixed = mixed.reshape(kv_count, tok_rows, group_size, HEAD_DIM).transpose(1, 0, 2, 3)
    attn = mixed.reshape(tok_rows, query_width).astype(jnp.bfloat16)
    layer_out = (stream[0].astype(jnp.float32) + attn.astype(jnp.float32)).astype(jnp.bfloat16)
    return passed_along(layer_out[None], "section", 1)


def solution(mesh):
    return jax.shard_map(
        shards,
        mesh=mesh,
        in_specs=(
            P("section", "seq", None),
            P("section", "seq", None),
            P("section", None, "seq", None),
            P("section", None, "seq", None),
            P(),
            P(),
            P(),
        ),
        out_specs=P("section", "seq", None),
        check_vma=False,
    )
```

profile of v0, /device:TPU:0, one launch (start us, length us, event | category | flops | bytes accessed | tf_op | source)
XLA Modules:
  0.0 129.9 jit_solution(16228814218623456433)
XLA Ops:
  6.5 0.0 copy-start
  6.5 0.0 all-gather.3.cloned.1.call-start
  6.5 1.6 %slice.31 = bf16[1,2,80,512]{3,2,1,0:T(8,128)(2,1)} slice(bf16[1,2,128,512]{3,2,1,0:T(8,128)(2,1)} %param.14), slice={[0:1], [0:2], [0:80], [0:512]} | slice | bytes 327680 | tf_op jit(solution)/shard_map/slice | solution.py:107
  8.2 0.0 copy-start.2
  8.2 0.0 all-gather.3.cloned.1.call-update
  8.2 0.0 all-gather.5.cloned.1.call-start
  8.2 1.8 %copy.27 = bf16[1,2,128,512]{2,3,1,0:T(8,128)(2,1)} copy(bf16[1,2,128,512]{3,2,1,0:T(8,128)(2,1)} %param.13) | data formatting | bytes 524288 | tf_op args[2]
  10.0 0.0 all-gather.5.cloned.1.call-update
  10.8 0.0 copy-done
  10.8 0.1 select_reduce_fusion.1
  10.9 1.4 %copy.32 = bf16[16,8,32,128]{3,2,1,0:T(8,128)(2,1)S(1)} copy(bf16[16,8,32,128]{3,1,2,0:T(8,128)(2,1)} %bitcast.80) | data formatting | bytes 2097152
  12.3 0.2 copy.41
  12.5 0.0 copy-done.2
  12.5 0.1 select_reduce_fusion.2
  12.6 22.5 %all-gather.3.cloned.1.call-done = bf16[1,2,640,512]{3,2,1,0:T(8,128)(2,1)} async-done(((bf16[1,2,80,512]{3,2,1,0:T(8,128)(2,1)}), bf16[1,2,640,512]{3,2,1,0:T(8,128)(2,1)}) %all-gather.3.cloned.1.call-update) | async-done | bytes 1310736 | tf_op jit(solution)/shard_map/all_gather | solution.py:110
  35.1 23.5 %while.37 = (s32[]{:T(128)}, f32[4,1024]{1,0:T(4,128)S(1)}, f32[4,1024]{1,0:T(4,128)S(1)}, f32[4,1024,128]{2,1,0:T(8,128)}, pred[640]{0:T(1024)(128)(4,1)S(1)}, ...) while((s32[]{:T(128)}, f32[4,1024]{1,0:T(4,128)S(1)}, ...), condition=%wide.region_4.5_spmd.clone, body=%wide.region_1.4_spmd.clone.sunk | while | flops 344346624 | bytes 15008751 | solution.py:72
  35.1 0.1 dynamic_slice.41
  35.2 1.0 constant_dynamic-slice_fusion.7
  36.3 0.5 select_reduce_fusion.4
  36.9 0.6 bitcast_reduce_fusion.2
  37.5 2.6 %fusion.61 = f32[4,1024,128]{2,1,0:T(8,128)} fusion(f32[4,1024,128]{2,1,0:T(8,128)} %get-tuple-element.492, f32[4,160,1024]{2,1,0:T(8,128)S(1)} %get-tuple-element.473, f32[4,1024]{1,0:T(4,128)S(1)} %select_maximum_fusion.2, pred[160]{0:T(512)(128)(4,1)S(1)} %dynamic_slice.41, f32[4,1024]{1,0:T(4,128)S(1)} %get-tuple-element.475, pred[]{:T(512)S(6)} %compare.7, ...), kind=kOutput, calls=%fused_computation.29.clone.1 | convolution fusion | flops 171966464 | bytes 7012513 | tf_op jit(solution)/shard_map/while/body/eval_jaxpr/kqr,rkd->kqd/dot_general | solution.py:50
  40.1 0.1 dynamic_slice.41
  40.1 1.0 constant_dynamic-slice_fusion.7
  41.2 0.6 select_reduce_fusion.4
  41.8 0.6 bitcast_reduce_fusion.2
  42.4 3.8 %fusion.61 = f32[4,1024,128]{2,1,0:T(8,128)} fusion(f32[4,1024,128]{2,1,0:T(8,128)} %get-tuple-element.492, f32[4,160,1024]{2,1,0:T(8,128)S(1)} %get-tuple-element.473, f32[4,1024]{1,0:T(4,128)S(1)} %select_maximum_fusion.2, pred[160]{0:T(512)(128)(4,1)S(1)} %dynamic_slice.41, f32[4,1024]{1,0:T(4,128)S(1)} %get-tuple-element.475, pred[]{:T(512)S(6)} %compare.7, ...), kind=kOutput, calls=%fused_computation.29.clone.1 | convolution fusion | flops 171966464 | bytes 7012513 | tf_op jit(solution)/shard_map/while/body/eval_jaxpr/kqr,rkd->kqd/dot_general | solution.py:50
  46.3 0.1 dynamic_slice.41
  46.3 1.0 constant_dynamic-slice_fusion.7
  47.4 0.5 select_reduce_fusion.4
  48.0 0.6 bitcast_reduce_fusion.2
  48.6 3.8 %fusion.61 = f32[4,1024,128]{2,1,0:T(8,128)} fusion(f32[4,1024,128]{2,1,0:T(8,128)} %get-tuple-element.492, f32[4,160,1024]{2,1,0:T(8,128)S(1)} %get-tuple-element.473, f32[4,1024]{1,0:T(4,128)S(1)} %select_maximum_fusion.2, pred[160]{0:T(512)(128)(4,1)S(1)} %dynamic_slice.41, f32[4,1024]{1,0:T(4,128)S(1)} %get-tuple-element.475, pred[]{:T(512)S(6)} %compare.7, ...), kind=kOutput, calls=%fused_computation.29.clone.1 | convolution fusion | flops 171966464 | bytes 7012513 | tf_op jit(solution)/shard_map/while/body/eval_jaxpr/kqr,rkd->kqd/dot_general | solution.py:50
  52.4 0.1 dynamic_slice.41
  52.5 1.0 constant_dynamic-slice_fusion.7
  53.6 0.5 select_reduce_fusion.4
  54.2 0.6 bitcast_reduce_fusion.2
  54.8 3.8 %fusion.61 = f32[4,1024,128]{2,1,0:T(8,128)} fusion(f32[4,1024,128]{2,1,0:T(8,128)} %get-tuple-element.492, f32[4,160,1024]{2,1,0:T(8,128)S(1)} %get-tuple-element.473, f32[4,1024]{1,0:T(4,128)S(1)} %select_maximum_fusion.2, pred[160]{0:T(512)(128)(4,1)S(1)} %dynamic_slice.41, f32[4,1024]{1,0:T(4,128)S(1)} %get-tuple-element.475, pred[]{:T(512)S(6)} %compare.7, ...), kind=kOutput, calls=%fused_computation.29.clone.1 | convolution fusion | flops 171966464 | bytes 7012513 | tf_op jit(solution)/shard_map/while/body/eval_jaxpr/kqr,rkd->kqd/dot_general | solution.py:50
  58.6 8.3 %all-gather.5.cloned.1.call-done = bf16[1,2,1024,512]{2,3,1,0:T(8,128)(2,1)} async-done(((bf16[1,2,128,512]{2,3,1,0:T(8,128)(2,1)}), bf16[1,2,1024,512]{2,3,1,0:T(8,128)(2,1)}) %all-gather.5.cloned.1.call-update) | async-done | bytes 2097168 | tf_op jit(solution)/shard_map/all_gather | solution.py:113
  66.9 23.6 %while.36 = (s32[]{:T(128)}, f32[4,1024]{1,0:T(4,128)S(1)}, f32[4,1024]{1,0:T(4,128)S(1)}, f32[4,1024,128]{2,1,0:T(8,128)}, pred[1024]{0:T(1024)(128)(4,1)S(1)},...) while((s32[]{:T(128)}, f32[4,1024]{1,0:T(4,128)S(1)}, ...), condition=%wide.region_9.10_spmd.clone, body=%wide.region_6.9_spmd.clone.sunk | while | flops 1097998976 | bytes 37100232 | solution.py:72
  66.9 0.1 dynamic_slice.40
  67.0 0.1 compare_and_fusion.2
  67.1 0.2 broadcast_bitcast_fusion.2
  67.3 0.9 copy.45
  68.3 1.3 constant_dynamic-slice_fusion.6
  69.6 1.8 %fusion.56 = (f32[4,1024]{1,0:T(4,128)S(1)}, f32[4,512,1024]{2,1,0:T(8,128)S(1)}) fusion(pred[1024,512]{0,1:T(8,128)(4,1)S(1)} %copy.45, bf16[512,4,128]{0,2,1:T(8,128)(2,1)S(1)} %bitcast.75, bf16[4,1024,128]{2,1,0:T(8,128)(2,1)S(1)} %get-tuple-element.545), kind=kOutput, calls=%fused_computation.3.clone.1 | convolution fusion | flops 543158272 | bytes 10502144 | tf_op jit(solution)/shard_map/while/body/eval_jaxpr/kqd,rkd->kqr/dot_general | solution.py:42
  71.4 1.8 %fusion.57 = f32[4,1024]{1,0:T(4,128)S(1)} fusion(f32[4,512,1024]{2,1,0:T(8,128)S(1)} %get-tuple-element.460, f32[4,1024]{1,0:T(4,128)S(1)} %max.19, pred[1024,512]{0,1:T(8,128)(4,1)S(1)} %copy.45), kind=kLoop, calls=%fused_computation.7.clone.1 | loop fusion | flops 8384512 | bytes 8945664 | tf_op jit(solution)/shard_map/while/body/eval_jaxpr/reduce_sum | solution.py:49
  73.3 5.4 %multiply_add_fusion.5 = f32[4,1024,128]{2,1,0:T(8,128)} fusion(f32[4,1024,128]{2,1,0:T(8,128)} %get-tuple-element.529, bf16[512,4,128]{0,2,1:T(8,128)(2,1)S(1)} %bitcast.77, f32[4,512,1024]{2,1,0:T(8,128)S(1)} %get-tuple-element.460, f32[4,1024]{1,0:T(4,128)S(1)} %max.19, pred[1024,512]{0,1:T(8,128)(4,1)S(1)} %copy.45, ...), kind=kOutput, calls=%fused_computation.13.clone.1 | convolution fusion | flops 546308096 | bytes 13664256 | tf_op jit(solution)/shard_map/while/body/eval_jaxpr/kqr,rkd->kqd/dot_general | solution.py:50
  78.7 0.1 dynamic_slice.40
  78.8 0.1 compare_and_fusion.2
  78.9 0.2 broadcast_bitcast_fusion.2
  79.1 0.9 copy.45
  80.1 1.3 constant_dynamic-slice_fusion.6
  81.4 1.8 %fusion.56 = (f32[4,1024]{1,0:T(4,128)S(1)}, f32[4,512,1024]{2,1,0:T(8,128)S(1)}) fusion(pred[1024,512]{0,1:T(8,128)(4,1)S(1)} %copy.45, bf16[512,4,128]{0,2,1:T(8,128)(2,1)S(1)} %bitcast.75, bf16[4,1024,128]{2,1,0:T(8,128)(2,1)S(1)} %get-tuple-element.545), kind=kOutput, calls=%fused_computation.3.clone.1 | convolution fusion | flops 543158272 | bytes 10502144 | tf_op jit(solution)/shard_map/while/body/eval_jaxpr/kqd,rkd->kqr/dot_general | solution.py:42
  83.2 1.8 %fusion.57 = f32[4,1024]{1,0:T(4,128)S(1)} fusion(f32[4,512,1024]{2,1,0:T(8,128)S(1)} %get-tuple-element.460, f32[4,1024]{1,0:T(4,128)S(1)} %max.19, pred[1024,512]{0,1:T(8,128)(4,1)S(1)} %copy.45), kind=kLoop, calls=%fused_computation.7.clone.1 | loop fusion | flops 8384512 | bytes 8945664 | tf_op jit(solution)/shard_map/while/body/eval_jaxpr/reduce_sum | solution.py:49
  85.1 5.4 %multiply_add_fusion.5 = f32[4,1024,128]{2,1,0:T(8,128)} fusion(f32[4,1024,128]{2,1,0:T(8,128)} %get-tuple-element.529, bf16[512,4,128]{0,2,1:T(8,128)(2,1)S(1)} %bitcast.77, f32[4,512,1024]{2,1,0:T(8,128)S(1)} %get-tuple-element.460, f32[4,1024]{1,0:T(4,128)S(1)} %max.19, pred[1024,512]{0,1:T(8,128)(4,1)S(1)} %copy.45, ...), kind=kOutput, calls=%fused_computation.13.clone.1 | convolution fusion | flops 546308096 | bytes 13664256 | tf_op jit(solution)/shard_map/while/body/eval_jaxpr/kqr,rkd->kqd/dot_general | solution.py:50
  90.5 2.0 %copy_bitcast_fusion = f32[128,4,8,128]{3,2,1,0:T(8,128)S(1)} fusion(f32[4,1024,128]{2,1,0:T(8,128)} %get-tuple-element.274, f32[4,1024]{1,0:T(4,128)S(1)} %get-tuple-element.275), kind=kLoop, calls=%fused_computation.45 | loop fusion | flops 1572864 | bytes 4210688 | tf_op jit(solution)/shard_map/convert_element_type | solution.py:118
  92.5 0.0 copy-start.1
  92.5 1.6 %reshape.106 = f32[1,128,4096]{2,1,0:T(8,128)} reshape(f32[128,4,8,128]{3,2,1,0:T(8,128)S(1)} %copy_bitcast_fusion) | data formatting | bytes 4194304 | tf_op jit(solution)/shard_map/convert_element_type | solution.py:118
  94.0 0.0 copy-done.1
  94.0 1.8 %add_convert_fusion = bf16[1,128,4096]{2,1,0:T(8,128)(2,1)S(1)} fusion(f32[1,128,4096]{2,1,0:T(8,128)} %reshape.106, bf16[1,128,4096]{2,1,0:T(8,128)(2,1)S(1)} %copy-done.1), kind=kLoop, calls=%fused_computation.46 | loop fusion | flops 1572864 | bytes 4194304 | tf_op jit(solution)/shard_map/convert_element_type | solution.py:118
  95.9 1.4 %collective-permute-start = (bf16[1,128,4096]{2,1,0:T(8,128)(2,1)S(1)}, bf16[1,128,4096]{2,1,0:T(8,128)(2,1)S(1)}, u32[]{:S(2)}, u32[]{:S(2)}) collective-permute-start(bf16[1,128,4096]{2,1,0:T(8,128)(2,1)S(1)} %add_convert_fusion), channel_id=1, source_target_pairs={{0,8},{8,16},{16,24},{24,0},{1,9},{9,17},{17,25},{25,1},{2,10},{10... | collective-permute-start | bytes 3145736 | tf_op jit(solution)/shard_map/ppermute | solution.py:15
  97.3 24.8 %collective-permute-done = bf16[1,128,4096]{2,1,0:T(8,128)(2,1)S(1)} collective-permute-done((bf16[1,128,4096]{2,1,0:T(8,128)(2,1)S(1)}, bf16[1,128,4096]{2,1,0:T(8,128)(2,1)S(1)}, u32[]{:S(2)}, u32[]{:S(2)}) %collective-permute-start) | collective-permute-done | bytes 1048608 | tf_op jit(solution)/shard_map/ppermute | solution.py:15
  122.1 1.0 copy.74
  (38 shorter events, 0.6 us)
Async XLA Ops:
  6.5 4.2 %copy-start = (s32[8,8]{1,0:T(8,128)S(1)}, s32[8,8]{1,0:T(8,128)}, u32[]{:S(2)}) copy-start(s32[8,8]{1,0:T(8,128)} %param.17) | copy-start | bytes 772
  6.5 28.6 %all-gather.3.cloned.1.call-start = ((), (), s32[]{:S(2)}) async-start(), calls=%async_computation | async-start | bytes 1474560 | tf_op jit(solution)/shard_map/all_gather | solution.py:110
  8.2 4.4 %copy-start.2 = (s32[8]{0:T(128)S(1)}, s32[8]{0:T(128)}, u32[]{:S(2)}) copy-start(s32[8]{0:T(128)} %param.15) | copy-start | bytes 100
  8.2 58.7 %all-gather.5.cloned.1.call-start = ((), (), s32[]{:S(2)}) async-start(), calls=%async_computation.1 | async-start | bytes 2359296 | tf_op jit(solution)/shard_map/all_gather | solution.py:113
  92.5 1.6 %copy-start.1 = (bf16[1,128,4096]{2,1,0:T(8,128)(2,1)S(1)}, bf16[1,128,4096]{2,1,0:T(8,128)(2,1)}, u32[]{:S(2)}) copy-start(bf16[1,128,4096]{2,1,0:T(8,128)(2,1)} %param.11) | copy-start | bytes 3145732
  95.9 26.2 %collective-permute-start = (bf16[1,128,4096]{2,1,0:T(8,128)(2,1)S(1)}, bf16[1,128,4096]{2,1,0:T(8,128)(2,1)S(1)}, u32[]{:S(2)}, u32[]{:S(2)}) collective-permute-start(bf16[1,128,4096]{2,1,0:T(8,128)(2,1)S(1)} %add_convert_fusion), channel_id=1, source_target_pairs={{0,8},{8,16},{16,24},{24,0},{1,9},{9,17},{17,25},{25,1},{2,10},{10... | collective-permute-start | bytes 3145736 | tf_op jit(solution)/shard_map/ppermute | solution.py:15
Sparse Core Ops, SparseCore 0:
  8.9 26.1 all-gather.2
  36.7 30.1 all-gather.4
where the time goes:
time: 131 us; the launch traced here: 130 us
  waiting for transfers between devices  55.6 us (42%)
  matrix products  30.6 us (23%)
  local copies, waits for them, and re-layouts  17.4 us (13%)
  between operations  14.2 us (11%)
  other arithmetic  10.4 us (8%)
  starting transfers between devices  1.49 us (1%)
    dot_general x6, matrix products, update(): jnp.einsum('kqr,rkd->kqd', weights.astype(jnp.bfloat16), value_heads, pre...  24.8 us
    ppermute x1, waiting for transfers between devices, passed_along(): return lax.ppermute(value, axis, pairs)  24.8 us
    all_gather x1, waiting for transfers between devices, shards(): lax.all_gather(live_slots, 'seq', axis=2, tiled=True)  22.5 us
    all_gather x1, waiting for transfers between devices, shards(): lax.all_gather(span_kv, 'seq', axis=2, tiled=True)  8.32 us
    slice x6, local copies, waits for them, and re-layouts, update(): value_heads = key_values[1].reshape(block_rows, kv_count, HEAD_DIM)  6.62 us
    reduce_sum x6, other arithmetic, update(): new_total = row_total * factor + jnp.sum(weights, -1)  5.97 us
    dot_general x6, matrix products, update(): jnp.einsum('kqd,rkd->kqr', grouped, key_heads, preferred_element_type=jnp...  5.83 us
    unnamed x9, local copies, waits for them, and re-layouts  4.22 us
  transfers between devices with their start and end apart: 3, of which 3 were waited for; matrix products, arithmetic and copies ran while one was open for 21% of the time, Pallas kernels for 0%

commit v1 on v0

v1 whole, which is shorter than its diff:
```python
import functools
import math

import jax
import jax.numpy as jnp
from jax import lax
from jax.experimental import pallas as pl
from jax.experimental.pallas import tpu as pltpu
from jax.sharding import PartitionSpec as P

HEAD_DIM = 128
LIVE_MAX = 80
TILE_HEADS = 2
CACHE, SPAN = 0, 1
UP, DOWN, SIDE = 0, 1, 2
MESH = pl.DeviceIdType.MESH


def kernel(
    seq_count, section_count, kv_count, group_size, tok_rows, slot_rows,
    len_ref, start_ref, table_ref, stream_hbm, query_hbm, span_hbm, cache_hbm,
    out_hbm,
    cache_all, span_all, query_v, stream_v, stage, cache_scores, span_scores,
    cache_bias, span_bias, top_v, acc_v,
    local_sem, bulk_sem, send_sem, recv_sem, hand_send, hand_recv,
):
    section = lax.axis_index("section")
    me = lax.axis_index("seq")
    chip_count = seq_count // 2
    chip = me // 2
    parity = me - chip * 2
    partner = me + 1 - 2 * parity
    has_up = chip < chip_count - 1
    has_down = chip > 0
    next_section = lax.rem(section + 1, section_count)
    prev_section = lax.rem(section + section_count - 1, section_count)
    tile_cols = TILE_HEADS * HEAD_DIM
    tile_rows = TILE_HEADS * tok_rows
    tiles_per = group_size // TILE_HEADS
    pair_keys = 2 * tok_rows
    cache_rows = seq_count * LIVE_MAX
    cache_chunk = math.gcd(seq_count, 8) * LIVE_MAX
    cache_chunks = cache_rows // cache_chunk

    def piece(kind, head, shard):
        if kind == CACHE:
            rows = pl.ds(pl.multiple_of(shard * LIVE_MAX, 16), LIVE_MAX)
            return cache_all.at[head, :, rows, :]
        rows = pl.ds(pl.multiple_of(shard * tok_rows, 16), tok_rows)
        return span_all.at[head, :, rows, :]

    def local_copy(kind, head):
        cols = pl.ds(pl.multiple_of(head * HEAD_DIM, HEAD_DIM), HEAD_DIM)
        if kind == CACHE:
            source = cache_hbm.at[0, :, pl.ds(0, LIVE_MAX), cols]
        else:
            source = span_hbm.at[0, :, :, cols]
        return pltpu.make_async_copy(source, piece(kind, head, me), local_sem.at[kind, head])

    def link(way, kind, head, shard):
        target = {UP: me + 2, DOWN: me - 2, SIDE: partner}[way]
        ref = piece(kind, head, shard)
        return pltpu.make_async_remote_copy(
            src_ref=ref, dst_ref=ref,
            send_sem=send_sem.at[way, kind, head, shard],
            recv_sem=recv_sem.at[kind, head, shard],
            device_id={"seq": target}, device_id_type=MESH,
        )

    def hand(tile):
        cols = pl.ds(pl.multiple_of(tile * tile_cols, tile_cols), tile_cols)
        return pltpu.make_async_remote_copy(
            src_ref=stage.at[:, cols], dst_ref=out_hbm.at[0, :, cols],
            send_sem=hand_send.at[tile], recv_sem=hand_recv.at[tile],
            device_id={"section": next_section}, device_id_type=MESH,
        )

    for head in range(kv_count):
        local_copy(CACHE, head).start()
        local_copy(SPAN, head).start()
    query_copy = pltpu.make_async_copy(query_hbm.at[0], query_v, bulk_sem.at[0])
    stream_copy = pltpu.make_async_copy(stream_hbm.at[0], stream_v, bulk_sem.at[1])
    query_copy.start()
    stream_copy.start()

    barrier = pltpu.get_barrier_semaphore()

    def greet(device):
        pl.semaphore_signal(barrier, inc=1, device_id=device, device_id_type=MESH)

    greet({"seq": partner})
    greet({"section": next_section})
    greet({"section": prev_section})

    @pl.when(has_up)
    def _():
        greet({"seq": me + 2})

    @pl.when(has_down)
    def _():
        greet({"seq": me - 2})

    key_col = lax.broadcasted_iota(jnp.int32, (1, cache_rows), 1)
    owner = jnp.zeros((1, cache_rows), jnp.int32)
    live = jnp.full((1, cache_rows), len_ref[0], jnp.int32)
    for shard in range(1, seq_count):
        later = key_col >= shard * LIVE_MAX
        owner = jnp.where(later, shard, owner)
        live = jnp.where(later, len_ref[shard], live)
    slot = key_col - owner * LIVE_MAX
    first_visible = slot_rows * seq_count - start_ref[0]
    cache_open = (slot < live) & (owner * slot_rows + slot >= first_visible)
    cache_bias[...] = jnp.where(cache_open, 0.0, -jnp.inf).astype(jnp.float32)
    pair_col = lax.broadcasted_iota(jnp.int32, (1, pair_keys), 1)
    for pair in range(chip_count):
        hits = jnp.where(pair_col < tok_rows, table_ref[me, 2 * pair], table_ref[me, 2 * pair + 1])
        span_bias[pair, :, :] = jnp.where(hits == 1, 0.0, -jnp.inf).astype(jnp.float32)

    pl.semaphore_wait(barrier, 3 + has_up.astype(jnp.int32) + has_down.astype(jnp.int32))

    def send_own(head):
        local_copy(CACHE, head).wait()
        local_copy(SPAN, head).wait()

        @pl.when(has_up)
        def _():
            link(UP, CACHE, head, me).start()
            link(UP, SPAN, head, me).start()

        @pl.when(has_down)
        def _():
            link(DOWN, CACHE, head, me).start()

        link(SIDE, CACHE, head, me).start()
        link(SIDE, SPAN, head, me).start()

    def relay(head):
        @pl.loop(1, chip_count)
        def _(step):
            @pl.when(step <= chip)
            def _():
                shard = me - 2 * step
                for kind in (CACHE, SPAN):
                    link(UP, kind, head, shard).wait_recv()

                    @pl.when(has_up)
                    def _():
                        link(UP, kind, head, shard).start()

                    link(SIDE, kind, head, shard).start()

            @pl.when(chip + step < chip_count)
            def _():
                shard = me + 2 * step
                link(DOWN, CACHE, head, shard).wait_recv()

                @pl.when(has_down)
                def _():
                    link(DOWN, CACHE, head, shard).start()

                link(SIDE, CACHE, head, shard).start()

    def from_partner(head):
        @pl.loop(0, chip_count)
        def _(other):
            shard = partner + 2 * (other - chip)
            link(SIDE, CACHE, head, shard).wait_recv()

            @pl.when(other <= chip)
            def _():
                link(SIDE, SPAN, head, shard).wait_recv()

    factor = math.log2(math.e) / math.sqrt(HEAD_DIM)

    def query_key(rows, keys):
        return lax.dot_general(
            rows, keys, (((1,), (1,)), ((), ())), preferred_element_type=jnp.float32
        )

    def lane_top(scores):
        best = scores[:, :HEAD_DIM]
        for first in range(HEAD_DIM, scores.shape[1], HEAD_DIM):
            best = jnp.maximum(best, scores[:, first : first + HEAD_DIM])
        return best

    def weighted(scores, row_top, values):
        weights = jnp.exp2((scores - row_top) * factor).astype(jnp.bfloat16)
        wide = jnp.concatenate([values, jnp.ones_like(values)], axis=1)
        return jnp.dot(weights, wide, preferred_element_type=jnp.float32)

    def cache_part(chunk):
        return pl.ds(pl.multiple_of(chunk * cache_chunk, 16), cache_chunk)

    def cache_lanes(chunk):
        if cache_chunks == 1:
            return pl.ds(0, cache_chunk)
        return pl.ds(pl.multiple_of(chunk * cache_chunk, HEAD_DIM), cache_chunk)

    def span_part(pair):
        return pl.ds(pl.multiple_of(pair * pair_keys, HEAD_DIM), pair_keys)

    def attend(head, tile):
        def cols(index):
            return pl.ds(pl.multiple_of((tile * TILE_HEADS + index) * HEAD_DIM, HEAD_DIM), HEAD_DIM)

        rows = jnp.concatenate([query_v[:, cols(i)] for i in range(TILE_HEADS)], axis=0)
        scores = query_key(rows, span_all[head, 0, span_part(chip), :]) + span_bias[chip]
        token = lax.broadcasted_iota(jnp.int32, (tok_rows, pair_keys), 0) + parity * tok_rows
        key = lax.broadcasted_iota(jnp.int32, (tok_rows, pair_keys), 1)
        causal = jnp.concatenate([key <= token] * TILE_HEADS, axis=0)
        scores = jnp.where(causal, scores, -jnp.inf)
        span_scores[:, span_part(chip)] = scores
        top_v[...] = lane_top(scores)

        def span_scored(pair, _):
            scores = query_key(rows, span_all[head, 0, span_part(pair), :]) + span_bias[pair]
            span_scores[:, span_part(pair)] = scores
            top_v[...] = jnp.maximum(top_v[...], lane_top(scores))
            return 0

        def cache_scored(chunk, _):
            scores = query_key(rows, cache_all[head, 0, cache_part(chunk), :])
            scores = scores + cache_bias[:, cache_lanes(chunk)]
            cache_scores[:, cache_lanes(chunk)] = scores
            top_v[...] = jnp.maximum(top_v[...], lane_top(scores))
            return 0

        lax.fori_loop(0, cache_chunks, cache_scored, 0)
        lax.fori_loop(0, chip, span_scored, 0)
        row_top = jnp.max(top_v[...], axis=1, keepdims=True)

        def cache_mixed(chunk, _):
            acc_v[...] += weighted(
                cache_scores[:, cache_lanes(chunk)], row_top, cache_all[head, 1, cache_part(chunk), :]
            )
            return 0

        def span_mixed(pair, _):
            acc_v[...] += weighted(
                span_scores[:, span_part(pair)], row_top, span_all[head, 1, span_part(pair), :]
            )
            return 0

        acc_v[...] = weighted(
            cache_scores[:, cache_lanes(0)], row_top, cache_all[head, 1, cache_part(0), :]
        )
        if cache_chunks > 1:
            lax.fori_loop(1, cache_chunks, cache_mixed, 0)
        lax.fori_loop(0, chip + 1, span_mixed, 0)
        attn = (acc_v[:, :HEAD_DIM] / acc_v[:, HEAD_DIM:]).astype(jnp.bfloat16).astype(jnp.float32)
        for index in range(TILE_HEADS):
            mixed = attn[index * tok_rows : (index + 1) * tok_rows]
            total = stream_v[:, cols(index)].astype(jnp.float32) + mixed
            stage[:, cols(index)] = total.astype(jnp.bfloat16)

    send_own(0)
    send_own(1)
    query_copy.wait()
    stream_copy.wait()

    @pl.loop(0, kv_count)
    def _(head):
        relay(head)

        @pl.when(head + 2 < kv_count)
        def _():
            send_own(head + 2)

        from_partner(head)

        @pl.loop(0, tiles_per)
        def _(part):
            tile = head * tiles_per + part
            attend(head, tile)

            @pl.when(tile > 0)
            def _():
                hand(tile - 1).start()

    @pl.loop(0, kv_count)
    def _(head):
        @pl.loop(0, chip_count)
        def _(other):
            shard = parity + 2 * other
            link(SIDE, CACHE, head, shard).wait_send()

            @pl.when(other <= chip)
            def _():
                link(SIDE, SPAN, head, shard).wait_send()

                @pl.when(has_up)
                def _():
                    link(UP, CACHE, head, shard).wait_send()
                    link(UP, SPAN, head, shard).wait_send()

            @pl.when((other >= chip) & has_down)
            def _():
                link(DOWN, CACHE, head, shard).wait_send()

    tile_count = kv_count * tiles_per
    hand(tile_count - 1).start()

    @pl.loop(0, tile_count)
    def _(tile):
        hand(tile).wait_recv()
        hand(tile).wait_send()


def shards(stream, queries, span_kv, cache_kv, cache_len, context_start, block_table):
    seq_count = lax.axis_size("seq")
    section_count = lax.axis_size("section")
    tok_rows, query_width = queries.shape[1:]
    key_width = span_kv.shape[3]
    kv_count = key_width // HEAD_DIM
    group_size = query_width // key_width
    slot_rows = cache_kv.shape[2]
    tile_rows = TILE_HEADS * tok_rows
    tile_count = kv_count * group_size // TILE_HEADS
    smem = pl.BlockSpec(memory_space=pltpu.SMEM)
    hbm = pl.BlockSpec(memory_space=pl.ANY)
    bf16, f32 = jnp.bfloat16, jnp.float32
    return pl.pallas_call(
        functools.partial(
            kernel, seq_count, section_count, kv_count, group_size, tok_rows, slot_rows
        ),
        out_shape=jax.ShapeDtypeStruct(stream.shape, bf16),
        in_specs=[smem] * 3 + [hbm] * 4,
        out_specs=hbm,
        scratch_shapes=[
            pltpu.VMEM((kv_count, 2, seq_count * LIVE_MAX, HEAD_DIM), bf16),
            pltpu.VMEM((kv_count, 2, seq_count * tok_rows, HEAD_DIM), bf16),
            pltpu.VMEM((tok_rows, query_width), bf16),
            pltpu.VMEM((tok_rows, query_width), bf16),
            pltpu.VMEM((tok_rows, query_width), bf16),
            pltpu.VMEM((tile_rows, seq_count * LIVE_MAX), f32),
            pltpu.VMEM((tile_rows, seq_count * tok_rows), f32),
            pltpu.VMEM((1, seq_count * LIVE_MAX), f32),
            pltpu.VMEM((seq_count // 2, 1, 2 * tok_rows), f32),
            pltpu.VMEM((tile_rows, HEAD_DIM), f32),
            pltpu.VMEM((tile_rows, 2 * HEAD_DIM), f32),
            pltpu.SemaphoreType.DMA((2, kv_count)),
            pltpu.SemaphoreType.DMA((2,)),
            pltpu.SemaphoreType.DMA((3, 2, kv_count, seq_count)),
            pltpu.SemaphoreType.DMA((2, kv_count, seq_count)),
            pltpu.SemaphoreType.DMA((tile_count,)),
            pltpu.SemaphoreType.DMA((tile_count,)),
        ],
        compiler_params=pltpu.CompilerParams(collective_id=0, has_side_effects=True),
    )(cache_len, context_start, block_table, stream, queries, span_kv, cache_kv)


def solution(mesh):
    return jax.shard_map(
        shards,
        mesh=mesh,
        in_specs=(
            P("section", "seq", None),
            P("section", "seq", None),
            P("section", None, "seq", None),
            P("section", None, "seq", None),
            P(),
            P(),
            P(),
        ),
        out_specs=P("section", "seq", None),
        check_vma=False,
    )
```

time: 131 us -> 66.3 us (0.51)
  the two profiles are of different devices: /device:TPU:0 before, /device:TPU:24 now
where the time goes in v1:
time: 66.3 us; the launch traced here: 66.1 us
  Pallas kernels  63.1 us (95%)
  local copies, waits for them, and re-layouts  2.29 us (3%)
    pallas_call x1, Pallas kernels, shards(): pl.pallas_call(functools.partial(kernel, seq_count, section_count, kv_cou...  63.1 us
    unnamed x1, local copies, waits for them, and re-layouts  2.29 us

profile of v1, /device:TPU:24, one launch (start us, length us, event | category | flops | bytes accessed | tf_op | source)
XLA Modules:
  0.0 66.1 jit_solution(12330166493149418550)
XLA Ops:
  0.7 63.1 %shard_map.73 = bf16[1,128,4096]{2,1,0:T(8,128)(2,1)} custom-call(s32[8]{0:T(128)} %len_ref.1, s32[1]{0:T(128)S(6)} %copy.9.start_ref, s32[8,8]{1,0:T(8,128)} %table_ref.1, bf16[1,128,4096]{2,1,0:T(8,128)(2,1)} %stream_hbm.1, bf16[1,128,4096]{2,1,0:T(8,128)(2,1)} %query_hbm.1, bf16[1,2,128,512]{3,2,1,0:T(8,128)(2,1)} %span_hbm.1, ...), custom_call_target="tpu_custom_call" | custom-call | tf_op jit(solution)/shard_map/pallas_call | solution.py:322
  63.8 2.3 %copy.10 = bf16[1,128,4096]{2,1,0:T(8,128)(2,1)} copy(bf16[1,128,4096]{2,1,0:T(8,128)(2,1)} %shard_map.73) | data formatting | bytes 2097152

commit v2 on v1

--- a/solution.py
+++ b/solution.py
@@ -11,6 +11,7 @@
 HEAD_DIM = 128
 LIVE_MAX = 80
 TILE_HEADS = 2
+BLOCK_HEADS = 8
 CACHE, SPAN = 0, 1
 UP, DOWN, SIDE = 0, 1, 2
 MESH = pl.DeviceIdType.MESH
@@ -35,8 +36,8 @@
     next_section = lax.rem(section + 1, section_count)
     prev_section = lax.rem(section + section_count - 1, section_count)
     tile_cols = TILE_HEADS * HEAD_DIM
-    tile_rows = TILE_HEADS * tok_rows
-    tiles_per = group_size // TILE_HEADS
+    tiles_per = BLOCK_HEADS // TILE_HEADS
+    blocks_per = group_size // BLOCK_HEADS
     pair_keys = 2 * tok_rows
     cache_rows = seq_count * LIVE_MAX
     cache_chunk = math.gcd(seq_count, 8) * LIVE_MAX
@@ -183,8 +184,9 @@
             best = jnp.maximum(best, scores[:, first : first + HEAD_DIM])
         return best
 
-    def weighted(scores, row_top, values):
-        weights = jnp.exp2((scores - row_top) * factor).astype(jnp.bfloat16)
+    def weighted(scores, values):
+        tops = jnp.concatenate([top_v[...]] * (scores.shape[1] // HEAD_DIM), axis=1)
+        weights = jnp.exp2((scores - tops) * factor).astype(jnp.bfloat16)
         wide = jnp.concatenate([values, jnp.ones_like(values)], axis=1)
         return jnp.dot(weights, wide, preferred_element_type=jnp.float32)
 
@@ -199,27 +201,30 @@
     def span_part(pair):
         return pl.ds(pl.multiple_of(pair * pair_keys, HEAD_DIM), pair_keys)
 
-    def attend(head, tile):
+    def attend(head, block):
         def cols(index):
-            return pl.ds(pl.multiple_of((tile * TILE_HEADS + index) * HEAD_DIM, HEAD_DIM), HEAD_DIM)
-
-        rows = jnp.concatenate([query_v[:, cols(i)] for i in range(TILE_HEADS)], axis=0)
-        scores = query_key(rows, span_all[head, 0, span_part(chip), :]) + span_bias[chip]
+            first = (block * BLOCK_HEADS + index) * HEAD_DIM
+            return pl.ds(pl.multiple_of(first, HEAD_DIM), HEAD_DIM)
+
+        def rows():
+            return jnp.concatenate([query_v[:, cols(i)] for i in range(BLOCK_HEADS)], axis=0)
+
+        scores = query_key(rows(), span_all[head, 0, span_part(chip), :]) + span_bias[chip]
         token = lax.broadcasted_iota(jnp.int32, (tok_rows, pair_keys), 0) + parity * tok_rows
         key = lax.broadcasted_iota(jnp.int32, (tok_rows, pair_keys), 1)
-        causal = jnp.concatenate([key <= token] * TILE_HEADS, axis=0)
+        causal = jnp.concatenate([key <= token] * BLOCK_HEADS, axis=0)
         scores = jnp.where(causal, scores, -jnp.inf)
         span_scores[:, span_part(chip)] = scores
         top_v[...] = lane_top(scores)
 
         def span_scored(pair, _):
-            scores = query_key(rows, span_all[head, 0, span_part(pair), :]) + span_bias[pair]
+            scores = query_key(rows(), span_all[head, 0, span_part(pair), :]) + span_bias[pair]
             span_scores[:, span_part(pair)] = scores
             top_v[...] = jnp.maximum(top_v[...], lane_top(scores))
             return 0
 
         def cache_scored(chunk, _):
-            scores = query_key(rows, cache_all[head, 0, cache_part(chunk), :])
+            scores = query_key(rows(), cache_all[head, 0, cache_part(chunk), :])
             scores = scores + cache_bias[:, cache_lanes(chunk)]
             cache_scores[:, cache_lanes(chunk)] = scores
             top_v[...] = jnp.maximum(top_v[...], lane_top(scores))
@@ -228,30 +233,36 @@
         lax.fori_loop(0, cache_chunks, cache_scored, 0)
         lax.fori_loop(0, chip, span_scored, 0)
         row_top = jnp.max(top_v[...], axis=1, keepdims=True)
-
-        def cache_mixed(chunk, _):
-            acc_v[...] += weighted(
-                cache_scores[:, cache_lanes(chunk)], row_top, cache_all[head, 1, cache_part(chunk), :]
-            )
+        top_v[...] = jnp.broadcast_to(row_top, top_v.shape)
+
+        def cache_mixed(chunk):
+            return weighted(cache_scores[:, cache_lanes(chunk)], cache_all[head, 1, cache_part(chunk), :])
+
+        def span_mixed(pair):
+            return weighted(span_scores[:, span_part(pair)], span_all[head, 1, span_part(pair), :])
+
+        def cache_added(chunk, _):
+            acc_v[...] += cache_mixed(chunk)
             return 0
 
-        def span_mixed(pair, _):
-            acc_v[...] += weighted(
-                span_scores[:, span_part(pair)], row_top, span_all[head, 1, span_part(pair), :]
-            )
+        def span_added(pair, _):
+            acc_v[...] += span_mixed(pair)
             return 0
 
-        acc_v[...] = weighted(
-            cache_scores[:, cache_lanes(0)], row_top, cache_all[head, 1, cache_part(0), :]
-        )
+        acc_v[...] = cache_mixed(0)
         if cache_chunks > 1:
-            lax.fori_loop(1, cache_chunks, cache_mixed, 0)
-        lax.fori_loop(0, chip + 1, span_mixed, 0)
-        attn = (acc_v[:, :HEAD_DIM] / acc_v[:, HEAD_DIM:]).astype(jnp.bfloat16).astype(jnp.float32)
+            lax.fori_loop(1, cache_chunks, cache_added, 0)
+        lax.fori_loop(0, chip + 1, span_added, 0)
+
+    def finish(tile, part):
         for index in range(TILE_HEADS):
-            mixed = attn[index * tok_rows : (index + 1) * tok_rows]
-            total = stream_v[:, cols(index)].astype(jnp.float32) + mixed
-            stage[:, cols(index)] = total.astype(jnp.bfloat16)
+            first = pl.multiple_of((part * TILE_HEADS + index) * tok_rows, tok_rows)
+            mixed = acc_v[pl.ds(first, tok_rows), :]
+            attn = (mixed[:, :HEAD_DIM] / mixed[:, HEAD_DIM:]).astype(jnp.bfloat16)
+            first = (tile * TILE_HEADS + index) * HEAD_DIM
+            cols = pl.ds(pl.multiple_of(first, HEAD_DIM), HEAD_DIM)
+            total = stream_v[:, cols].astype(jnp.float32) + attn.astype(jnp.float32)
+            stage[:, cols] = total.astype(jnp.bfloat16)
 
     send_own(0)
     send_own(1)
@@ -268,14 +279,19 @@
 
         from_partner(head)
 
-        @pl.loop(0, tiles_per)
-        def _(part):
-            tile = head * tiles_per + part
-            attend(head, tile)
-
-            @pl.when(tile > 0)
-            def _():
-                hand(tile - 1).start()
+        @pl.loop(0, blocks_per)
+        def _(inner):
+            block = head * blocks_per + inner
+            attend(head, block)
+
+            @pl.loop(0, tiles_per)
+            def _(part):
+                tile = block * tiles_per + part
+                finish(tile, part)
+
+                @pl.when(tile > 0)
+                def _():
+                    hand(tile - 1).start()
 
     @pl.loop(0, kv_count)
     def _(head):
@@ -297,7 +313,7 @@
             def _():
                 link(DOWN, CACHE, head, shard).wait_send()
 
-    tile_count = kv_count * tiles_per
+    tile_count = kv_count * group_size // TILE_HEADS
     hand(tile_count - 1).start()
 
     @pl.loop(0, tile_count)
@@ -314,7 +330,7 @@
     kv_count = key_width // HEAD_DIM
     group_size = query_width // key_width
     slot_rows = cache_kv.shape[2]
-    tile_rows = TILE_HEADS * tok_rows
+    block_rows = BLOCK_HEADS * tok_rows
     tile_count = kv_count * group_size // TILE_HEADS
     smem = pl.BlockSpec(memory_space=pltpu.SMEM)
     hbm = pl.BlockSpec(memory_space=pl.ANY)
@@ -332,12 +348,12 @@
             pltpu.VMEM((tok_rows, query_width), bf16),
             pltpu.VMEM((tok_rows, query_width), bf16),
             pltpu.VMEM((tok_rows, query_width), bf16),
-            pltpu.VMEM((tile_rows, seq_count * LIVE_MAX), f32),
-            pltpu.VMEM((tile_rows, seq_count * tok_rows), f32),
+            pltpu.VMEM((block_rows, seq_count * LIVE_MAX), f32),
+            pltpu.VMEM((block_rows, seq_count * tok_rows), f32),
             pltpu.VMEM((1, seq_count * LIVE_MAX), f32),
             pltpu.VMEM((seq_count // 2, 1, 2 * tok_rows), f32),
-            pltpu.VMEM((tile_rows, HEAD_DIM), f32),
-            pltpu.VMEM((tile_rows, 2 * HEAD_DIM), f32),
+            pltpu.VMEM((block_rows, HEAD_DIM), f32),
+            pltpu.VMEM((block_rows, 2 * HEAD_DIM), f32),
             pltpu.SemaphoreType.DMA((2, kv_count)),
             pltpu.SemaphoreType.DMA((2,)),
             pltpu.SemaphoreType.DMA((3, 2, kv_count, seq_count)),

time: 66.3 us -> 56.7 us (0.86)
  the two profiles are of different devices: /device:TPU:24 before, /device:TPU:0 now
where the time goes in v2:
time: 56.7 us; the launch traced here: 56.5 us
  Pallas kernels  53.5 us (94%)
  local copies, waits for them, and re-layouts  2.29 us (4%)
  between operations  0.66 us (1%)
    pallas_call x1, Pallas kernels, shards(): pl.pallas_call(functools.partial(kernel, seq_count, section_count, kv_cou...  53.5 us
    unnamed x1, local copies, waits for them, and re-layouts  2.29 us

profile of v2, /device:TPU:0, one launch (start us, length us, event | category | flops | bytes accessed | tf_op | source)
XLA Modules:
  0.0 56.5 jit_solution(18418864696647106663)
XLA Ops:
  0.7 53.5 %shard_map.73 = bf16[1,128,4096]{2,1,0:T(8,128)(2,1)} custom-call(s32[8]{0:T(128)} %len_ref.1, s32[1]{0:T(128)S(6)} %copy.9.start_ref, s32[8,8]{1,0:T(8,128)} %table_ref.1, bf16[1,128,4096]{2,1,0:T(8,128)(2,1)} %stream_hbm.1, bf16[1,128,4096]{2,1,0:T(8,128)(2,1)} %query_hbm.1, bf16[1,2,128,512]{3,2,1,0:T(8,128)(2,1)} %span_hbm.1, ...), custom_call_target="tpu_custom_call" | custom-call | tf_op jit(solution)/shard_map/pallas_call | solution.py:338
  54.2 2.3 %copy.10 = bf16[1,128,4096]{2,1,0:T(8,128)(2,1)} copy(bf16[1,128,4096]{2,1,0:T(8,128)(2,1)} %shard_map.73) | data formatting | bytes 2097152
